TPU v7x, 32 devices: a whole 2x2x4 slice. The times are simulated.
32 devices in a mesh: space: 8 (over z, x), rad: 4 (over y, core).
Axes of the slice: x: 2, y: 2, z: 4, core: 2. Of those that a mesh axis runs over, the one named last changes fastest.
Arguments:
- cell_bin: int32 [524288], P(('space', 'rad')), may hold values from 0 to 255
- cell_fields: float32 [3, 524288], P(None, ('space', 'rad')), may hold values from 0.0005 to 0.005
- tile_halo: int32 [4096], P(('space', 'rad')), may hold values from 0 to 255, as said below
- halo_owner: int32 [256], replicated, may hold values from 0 to 7, as said below
Outputs:
- enclosed_mass: float32 [256, 256], P('space', 'rad')
- enclosed_volume: float32 [256, 256], P('space', 'rad')
- cumulative_entropy: float32 [256, 256], P('space', 'rad')
- circular_velocity: float32 [256, 256], P('space', 'rad')
Inputs may be any that keep to these rules, and one draw needn't show every extreme that they name: `tile_halo`: the tiles of one device are in nondecreasing halo order; they go to exactly 4 owners, 32 tiles to each; the tiles of one device with one owner hold at most 16 distinct halos, and on every device some owner receives exactly 16. `halo_owner`: each index of space owns 32 consecutive halo ids.
All inputs are finite; a program needn't handle non-finite values.
Results may differ from a plain program's by a relative error of at most 0.000067.
Values sent between devices are 32-bit elements; how exact they have to be, the bound alone decides.
No kernel may reach another device: no remote copies, remote signals or barrier semaphores. Data moves between devices by JAX's collectives and lax.ppermute only.
A program may use at most 64 MiB of HBM per device.

v0:
```python
import math

import jax
import jax.numpy as jnp
from jax import lax
from jax.sharding import PartitionSpec as P

TILE = 128
BINS = 256


log_inner = -2.302585092994046


def prefix(part, axis, combine, identity):
    place = lax.axis_index(axis)
    gathered = lax.all_gather(part, axis)
    state = jnp.zeros_like(part) + jnp.asarray(identity, part.dtype)

    def one(lap, state):
        return combine(state, lax.dynamic_index_in_dim(gathered, lap, 0, False))

    return lax.fori_loop(0, place, one, state)


def bin_tiles(cell_bin, cell_fields, tile_count):
    group_size = math.gcd(tile_count, 16)
    groups = tile_count // group_size
    bin_labels = cell_bin.reshape(groups, group_size, TILE)
    fields = cell_fields.reshape(3, groups, group_size, TILE).transpose(1, 0, 2, 3)
    bin_ids = jnp.arange(BINS, dtype=jnp.int32)

    def one_group(pair):
        labels, values = pair
        onehot = (labels[:, :, None] == bin_ids[None, None, :]).astype(jnp.float32)
        return jnp.einsum("ftc,tcb->tfb", values, onehot, precision=lax.Precision.HIGHEST)

    result = lax.map(one_group, (bin_labels, fields))
    return result.reshape(tile_count, 3 * BINS)


def pack_slots(pieces, target, slot_rank, slot_count, weights, spaces):
    slot_pos = target * slot_count + slot_rank
    placer = (
        slot_pos[:, None] == jnp.arange(spaces * slot_count, dtype=jnp.int32)[None, :]
    ).astype(jnp.float32)
    outgoing = jnp.dot(
        placer.T, pieces, precision=lax.Precision.HIGHEST, preferred_element_type=jnp.float32
    )
    slot_tags = (
        jnp.dot(
            weights, placer, precision=lax.Precision.HIGHEST, preferred_element_type=jnp.float32
        )
        - 1.0
    )
    return (outgoing.reshape(spaces, slot_count, 3 * BINS), slot_tags.reshape(spaces, slot_count))


def collect(received, got_tags, halo_dev, width):
    slot_rows = got_tags.size
    receiver = (
        got_tags.reshape(slot_rows)[:, None] == jnp.arange(halo_dev, dtype=jnp.float32)[None, :]
    ).astype(jnp.float32)
    return jnp.dot(
        receiver.T,
        received.reshape(slot_rows, width),
        precision=lax.Precision.HIGHEST,
        preferred_element_type=jnp.float32,
    )


def body(cell_bin, cell_fields, tile_halo, halo_owner):
    spaces = lax.axis_size("space")
    rads = lax.axis_size("rad")
    bin_dev = BINS // rads
    tile_count = tile_halo.shape[0]
    halo_dev = halo_owner.shape[0] // spaces
    capacity = max(2, 2 * tile_count // spaces)
    pieces = bin_tiles(cell_bin, cell_fields, tile_count)
    owner_hot = (halo_owner[:, None] == jnp.arange(spaces, dtype=jnp.int32)[None, :]).astype(
        jnp.int32
    )
    local_rank = jnp.sum((jnp.cumsum(owner_hot, axis=0) - owner_hot) * owner_hot, axis=1)
    target = halo_owner[tile_halo]
    labels = local_rank[tile_halo].astype(jnp.float32) + 1.0
    matches = (target[:, None] == target[None, :]).astype(jnp.int32)
    positions = jnp.arange(tile_count, dtype=jnp.int32)
    starts = jnp.concatenate(
        [jnp.ones((1,), jnp.int32), (tile_halo[1:] != tile_halo[:-1]).astype(jnp.int32)]
    )
    through = (positions[:, None] <= positions[None, :]).astype(jnp.int32)
    slot_rank = jnp.sum(matches * through * starts[:, None], axis=0) - 1
    slot_count = max(1, capacity // 2)
    outgoing, slot_tags = pack_slots(
        pieces, target, slot_rank, slot_count, labels * starts.astype(jnp.float32), spaces
    )
    received, got_tags = (
        lax.all_to_all(outgoing, "space", split_axis=0, concat_axis=0, tiled=True),
        lax.all_to_all(slot_tags, "space", split_axis=0, concat_axis=0, tiled=True),
    )
    owned = collect(received, got_tags, halo_dev, 3 * BINS)
    shares = lax.psum_scatter(
        owned.reshape(halo_dev, 3, BINS), "rad", scatter_dimension=2, tiled=True
    )
    running = jnp.cumsum(shares, axis=2)
    totals = running[:, :, -1]
    offset = prefix(totals, "rad", jnp.add, jnp.zeros_like(totals))
    running = running + offset[:, :, None]
    global_bin = lax.axis_index("rad") * bin_dev + jnp.arange(bin_dev, dtype=jnp.int32) + 1
    radius = jnp.exp(log_inner + global_bin.astype(jnp.float32) * (-log_inner / BINS))
    enclosed = running[:, 0, :]
    return (enclosed, running[:, 1, :], running[:, 2, :], jnp.sqrt(enclosed / radius[None, :]))


def solution(mesh):
    in_specs = (P(("space", "rad")), P(None, ("space", "rad")), P(("space", "rad")), P())
    out_specs = (P("space", "rad"), P("space", "rad"), P("space", "rad"), P("space", "rad"))
    return jax.shard_map(body, mesh=mesh, in_specs=in_specs, out_specs=out_specs, check_vma=False)
```

profile of v0, /device:TPU:0, one launch (start us, length us, event | category | flops | bytes accessed | tf_op | source)
XLA Modules:
  0.0 93.8 jit_solution(16456237956290326786)
XLA Ops:
  7.2 0.0 copy-start
  7.2 0.7 compare_select_fusion
  7.8 0.8 slice_compare_fusion
  8.7 1.6 %gather_fusion.1 = s32[128]{0:T(128)S(1)} fusion(s32[256]{0:T(256)} %param.11, s32[1024]{0:T(1024)S(1)} %pad_clamp_fusion), kind=kCustom, calls=%fused_computation.1 | custom fusion | bytes 1536 | tf_op jit(solution)/shard_map/gather | solution.py:84
  10.3 0.1 add_convert_fusion
  10.4 0.1 multiply_reduce_fusion
  10.5 0.0 copy-done
  10.5 0.6 reduce-window.6
  11.1 0.2 slice_reduce_fusion
  11.4 0.1 fusion.20
  11.5 1.3 %gather_fusion = s32[128]{0:T(128)S(1)} fusion(s32[256]{0:T(256)S(1)} %fusion.20, s32[1024]{0:T(1024)S(1)} %pad_clamp_fusion), kind=kCustom, calls=%fused_computation | custom fusion | bytes 1536 | tf_op jit(solution)/shard_map/gather | solution.py:85
  12.7 0.2 fusion.10
  12.9 0.7 all_to_all.9
  13.6 7.3 %all-to-all-start = ((f32[8,1,16]{2,1,0:T(1,128)}), f32[8,1,16]{2,1,0:T(1,128)S(1)}, u32[]{:S(2)}, u32[]{:S(2)}) async-start(f32[8,1,16]{2,1,0:T(1,128)} %bitcast.6), calls=%async_computation | async-start | bytes 8192 | tf_op jit(solution)/shard_map/all_to_all | solution.py:99
  20.9 18.1 %while.22 = (s32[]{:T(128)}, f32[8,16,3,256]{3,2,1,0:T(4,128)S(1)}, f32[8,3,16,128]{3,1,2,0:T(4,128)}, s32[8,16,128]{2,1,0:T(8,128)}, s32[]{:T(128)}) while((s32[]{:T(128)}, f32[8,16,3,256]{3,2,1,0:T(4,128)S(1)}, f32[8,3,16,128]{3,1,2,0:T(4,128)}, s32[8,16,128]{2,1,0:T(8,128)}, s32[]{:T(128)}) %tuple.53), condition=%wide.region_5.6_spmd.clone, body=%wide.region_4.5_spmd.clone.sunk | while | flops 19398656 | bytes 123969 | solution.py:38
  20.9 0.7 dynamic-slice_bitcast_fusion.2
  21.6 1.6 %fusion.37 = f32[8,16,3,256]{3,2,1,0:T(4,128)S(1)} fusion(f32[8,16,3,256]{3,2,1,0:T(4,128)S(1)} %get-tuple-element.159, s32[]{:T(128)} %get-tuple-element.158, s32[16,128]{1,0:T(8,128)S(1)} %dynamic-slice_bitcast_fusion.2, f32[8,3,16,128]{3,1,2,0:T(4,128)} %get-tuple-element.165), kind=kOutput, calls=%fused_computation.9.clone.1 | convolution fusion | flops 19398656 | bytes 107520 | tf_op jit(solution)/shard_map/while/body/eval_jaxpr/ftc,tcb->tfb/dot_general | solution.py:36
  23.2 0.7 dynamic-slice_bitcast_fusion.2
  23.9 1.6 %fusion.37 = f32[8,16,3,256]{3,2,1,0:T(4,128)S(1)} fusion(f32[8,16,3,256]{3,2,1,0:T(4,128)S(1)} %get-tuple-element.159, s32[]{:T(128)} %get-tuple-element.158, s32[16,128]{1,0:T(8,128)S(1)} %dynamic-slice_bitcast_fusion.2, f32[8,3,16,128]{3,1,2,0:T(4,128)} %get-tuple-element.165), kind=kOutput, calls=%fused_computation.9.clone.1 | convolution fusion | flops 19398656 | bytes 107520 | tf_op jit(solution)/shard_map/while/body/eval_jaxpr/ftc,tcb->tfb/dot_general | solution.py:36
  25.4 0.7 dynamic-slice_bitcast_fusion.2
  26.2 1.6 %fusion.37 = f32[8,16,3,256]{3,2,1,0:T(4,128)S(1)} fusion(f32[8,16,3,256]{3,2,1,0:T(4,128)S(1)} %get-tuple-element.159, s32[]{:T(128)} %get-tuple-element.158, s32[16,128]{1,0:T(8,128)S(1)} %dynamic-slice_bitcast_fusion.2, f32[8,3,16,128]{3,1,2,0:T(4,128)} %get-tuple-element.165), kind=kOutput, calls=%fused_computation.9.clone.1 | convolution fusion | flops 19398656 | bytes 107520 | tf_op jit(solution)/shard_map/while/body/eval_jaxpr/ftc,tcb->tfb/dot_general | solution.py:36
  27.7 0.7 dynamic-slice_bitcast_fusion.2
  28.4 1.6 %fusion.37 = f32[8,16,3,256]{3,2,1,0:T(4,128)S(1)} fusion(f32[8,16,3,256]{3,2,1,0:T(4,128)S(1)} %get-tuple-element.159, s32[]{:T(128)} %get-tuple-element.158, s32[16,128]{1,0:T(8,128)S(1)} %dynamic-slice_bitcast_fusion.2, f32[8,3,16,128]{3,1,2,0:T(4,128)} %get-tuple-element.165), kind=kOutput, calls=%fused_computation.9.clone.1 | convolution fusion | flops 19398656 | bytes 107520 | tf_op jit(solution)/shard_map/while/body/eval_jaxpr/ftc,tcb->tfb/dot_general | solution.py:36
  30.0 0.7 dynamic-slice_bitcast_fusion.2
  30.7 1.6 %fusion.37 = f32[8,16,3,256]{3,2,1,0:T(4,128)S(1)} fusion(f32[8,16,3,256]{3,2,1,0:T(4,128)S(1)} %get-tuple-element.159, s32[]{:T(128)} %get-tuple-element.158, s32[16,128]{1,0:T(8,128)S(1)} %dynamic-slice_bitcast_fusion.2, f32[8,3,16,128]{3,1,2,0:T(4,128)} %get-tuple-element.165), kind=kOutput, calls=%fused_computation.9.clone.1 | convolution fusion | flops 19398656 | bytes 107520 | tf_op jit(solution)/shard_map/while/body/eval_jaxpr/ftc,tcb->tfb/dot_general | solution.py:36
  32.2 0.7 dynamic-slice_bitcast_fusion.2
  32.9 1.6 %fusion.37 = f32[8,16,3,256]{3,2,1,0:T(4,128)S(1)} fusion(f32[8,16,3,256]{3,2,1,0:T(4,128)S(1)} %get-tuple-element.159, s32[]{:T(128)} %get-tuple-element.158, s32[16,128]{1,0:T(8,128)S(1)} %dynamic-slice_bitcast_fusion.2, f32[8,3,16,128]{3,1,2,0:T(4,128)} %get-tuple-element.165), kind=kOutput, calls=%fused_computation.9.clone.1 | convolution fusion | flops 19398656 | bytes 107520 | tf_op jit(solution)/shard_map/while/body/eval_jaxpr/ftc,tcb->tfb/dot_general | solution.py:36
  34.5 0.7 dynamic-slice_bitcast_fusion.2
  35.2 1.6 %fusion.37 = f32[8,16,3,256]{3,2,1,0:T(4,128)S(1)} fusion(f32[8,16,3,256]{3,2,1,0:T(4,128)S(1)} %get-tuple-element.159, s32[]{:T(128)} %get-tuple-element.158, s32[16,128]{1,0:T(8,128)S(1)} %dynamic-slice_bitcast_fusion.2, f32[8,3,16,128]{3,1,2,0:T(4,128)} %get-tuple-element.165), kind=kOutput, calls=%fused_computation.9.clone.1 | convolution fusion | flops 19398656 | bytes 107520 | tf_op jit(solution)/shard_map/while/body/eval_jaxpr/ftc,tcb->tfb/dot_general | solution.py:36
  36.7 0.7 dynamic-slice_bitcast_fusion.2
  37.5 1.6 %fusion.37 = f32[8,16,3,256]{3,2,1,0:T(4,128)S(1)} fusion(f32[8,16,3,256]{3,2,1,0:T(4,128)S(1)} %get-tuple-element.159, s32[]{:T(128)} %get-tuple-element.158, s32[16,128]{1,0:T(8,128)S(1)} %dynamic-slice_bitcast_fusion.2, f32[8,3,16,128]{3,1,2,0:T(4,128)} %get-tuple-element.165), kind=kOutput, calls=%fused_computation.9.clone.1 | convolution fusion | flops 19398656 | bytes 107520 | tf_op jit(solution)/shard_map/while/body/eval_jaxpr/ftc,tcb->tfb/dot_general | solution.py:36
  39.0 0.3 reshape.111
  39.3 1.1 %fusion.11 = f32[8,16,768]{2,1,0:T(8,128)} fusion(f32[128,768,1]{1,0,2:T(8,128)S(1)} %reshape.111, s32[8,16]{1,0:T(8,128)S(1)} %multiply_add_fusion, s32[128]{0:T(128)S(1)} %add_add_fusion), kind=kOutput, calls=%fused_computation.20 | convolution fusion | flops 151011328 | bytes 787456 | tf_op jit(solution)/shard_map/dot_general | solution.py:47
  40.4 0.0 all-to-all-done
  40.4 6.0 %all-to-all-start.1 = ((f32[8,16,768]{2,1,0:T(8,128)}), f32[8,16,768]{2,1,0:T(8,128)S(1)}, u32[]{:S(2)}, u32[]{:S(2)}) async-start(f32[8,16,768]{2,1,0:T(8,128)} %fusion.11), calls=%async_computation.1 | async-start | bytes 786432 | tf_op jit(solution)/shard_map/all_to_all | solution.py:98
  46.4 0.0 reduce-scatter.4.cloned.1.call-start
  46.4 0.5 broadcast.113
  46.9 0.7 reduce.6
  47.6 0.1 eq.99
  47.7 9.8 %all-to-all-done.1 = f32[8,16,768]{2,1,0:T(8,128)S(1)} async-done(((f32[8,16,768]{2,1,0:T(8,128)}), f32[8,16,768]{2,1,0:T(8,128)S(1)}, u32[]{:S(2)}, u32[]{:S(2)}) %all-to-all-start.1) | async-done | bytes 393248 | tf_op jit(solution)/shard_map/all_to_all | solution.py:98
  57.5 0.2 copy.16
  57.7 0.3 fusion.17
  58.0 0.2 copy.18
  58.2 0.9 reshape.114
  59.1 0.0 reduce-scatter.4.cloned.1.call-update
  59.2 18.9 %reduce-scatter.4.cloned.1.call-done = f32[64,96]{1,0:T(8,128)} async-done(((f32[256,96]{1,0:T(8,128)}), f32[64,96]{1,0:T(8,128)}) %reduce-scatter.4.cloned.1.call-update) | async-done | bytes 24592
  78.0 0.9 reshape.115
  78.9 0.1 copy.19
  79.0 0.7 reduce_window_sum.28
  79.7 0.1 slice.37
  79.8 5.6 %all-gather = f32[128,3,1]{2,0,1:T(8,128)S(1)} all-gather(f32[32,3,1]{2,0,1:T(8,128)S(1)} %slice.37), channel_id=2, replica_groups=mesh['space'=8,'rad'=4] {'rad'}, dimensions={0}, use_global_device_ids=true | all-gather | bytes 1920 | tf_op jit(solution)/shard_map/all_gather | solution.py:17
  85.4 0.1 reduce.2
  85.5 0.1 reshape.106
  85.6 0.1 broadcast_add_fusion
  85.7 0.6 slice_bitcast_fusion
  86.3 0.6 divide_sqrt_fusion
  (10 shorter events, 0.1 us)
Async XLA Ops:
  7.2 3.3 %copy-start = (s32[256]{0:T(256)S(1)}, s32[256]{0:T(256)}, u32[]{:S(2)}) copy-start(s32[256]{0:T(256)} %param.11) | copy-start | bytes 3076
  13.6 26.8 %all-to-all-start = ((f32[8,1,16]{2,1,0:T(1,128)}), f32[8,1,16]{2,1,0:T(1,128)S(1)}, u32[]{:S(2)}, u32[]{:S(2)}) async-start(f32[8,1,16]{2,1,0:T(1,128)} %bitcast.6), calls=%async_computation | async-start | bytes 8192 | tf_op jit(solution)/shard_map/all_to_all | solution.py:99
  40.4 17.1 %all-to-all-start.1 = ((f32[8,16,768]{2,1,0:T(8,128)}), f32[8,16,768]{2,1,0:T(8,128)S(1)}, u32[]{:S(2)}, u32[]{:S(2)}) async-start(f32[8,16,768]{2,1,0:T(8,128)} %fusion.11), calls=%async_computation.1 | async-start | bytes 786432 | tf_op jit(solution)/shard_map/all_to_all | solution.py:98
  46.4 31.7 %reduce-scatter.4.cloned.1.call-start = ((), (), s32[]{:S(2)}) async-start(), calls=%async_computation.3 | async-start | bytes 163840
Sparse Core Ops, SparseCore 0:
  59.3 18.7 reduce-scatter.3
where the time goes:
time: 95 us; the launch traced here: 93.8 us
  waiting for transfers between devices  28.7 us (30%)
  between operations  14.1 us (15%)
  matrix products  14 us (15%)
  local copies, waits for them, and re-layouts  13.4 us (14%)
  starting transfers between devices  13.3 us (14%)
  blocking collectives  5.6 us (6%)
  other arithmetic  4.6 us (5%)
    unnamed x2, waiting for transfers between devices  18.9 us
    dot_general x8, matrix products, one_group(): jnp.einsum('ftc,tcb->tfb', values, onehot, precision=lax.Precision.HIGHEST)  12.4 us
    all_to_all x1, waiting for transfers between devices, body(): lax.all_to_all(outgoing, 'space', split_axis=0, concat_axis=0, tiled=True)  9.82 us
    all_to_all x1, starting transfers between devices, body(): lax.all_to_all(slot_tags, 'space', split_axis=0, concat_axis=0, tiled=True)  7.28 us
    all_to_all x1, starting transfers between devices, body(): lax.all_to_all(outgoing, 'space', split_axis=0, concat_axis=0, tiled=True)  5.98 us
    eq x8, local copies, waits for them, and re-layouts, one_group(): onehot = (labels[:, :, None] == bin_ids[None, None, :]).astype(jnp.float32)  5.65 us
    all_gather x1, blocking collectives, prefix(): gathered = lax.all_gather(part, axis)  5.6 us
    unnamed x6, local copies, waits for them, and re-layouts  2.05 us
  transfers between devices with their start and end apart: 3, of which 2 were waited for; matrix products, arithmetic and copies ran while one was open for 22% of the time, Pallas kernels for 0%

commit v1 on v0

v1 whole, which is shorter than its diff:
```python
import functools
import math

import jax
import jax.numpy as jnp
from jax import lax
from jax.experimental import pallas as pl
from jax.experimental.pallas import tpu as pltpu
from jax.sharding import PartitionSpec as P

TILE = 128
BINS = 256
LANES = 128
PACK = 16
CHUNK = 8
BATCH = 32
VMEM_LIMIT = 16 * 1024 * 1024

log_inner = -2.302585092994046


def split(x):
    hi = x.astype(jnp.bfloat16).astype(jnp.float32)
    return hi, x - hi


def bin_kernel(spaces, rads, per, slots, rows, owner_ref, halo_ref, bin_ref, field_ref, out_ref):
    tiles = bin_ref.shape[0]
    halo_dev = owner_ref.shape[0] // spaces
    bin_dev = BINS // rads
    parts = LANES // bin_dev
    sub = slots // parts
    one, zero = jnp.bfloat16(1), jnp.bfloat16(0)
    bin_ids = [
        (lax.broadcasted_iota(jnp.int32, (PACK, LANES), 0) + k * PACK).astype(jnp.float32).astype(jnp.bfloat16)
        for k in range(BINS // PACK)
    ]
    slot_ids = lax.broadcasted_iota(jnp.int32, (slots, LANES), 0)
    lane = lax.broadcasted_iota(jnp.int32, (1, LANES), 1)

    @pl.loop(0, spaces * rads)
    def _(block):
        out_ref[pl.ds(block * rows, rows - 1), 0, :] = jnp.zeros((rows - 1, LANES), jnp.float32)
        out_ref[block * rows + rows - 1] = jnp.full((1, LANES), -1.0, jnp.float32)

    @pl.loop(0, tiles // per)
    def _(group):
        owner = owner_ref[halo_ref[group * per]]
        slot = jnp.int32(0)
        places = jnp.full((1, LANES), -1, jnp.int32)
        total = None
        for chunk in range(0, per, CHUNK):
            steps, values = [], []
            for k in range(chunk, min(chunk + CHUNK, per)):
                t = group * per + k
                halo = halo_ref[t]
                if k:
                    slot = slot + (halo != halo_ref[t - 1]).astype(jnp.int32)
                local = lax.rem(halo, halo_dev)
                places = jnp.where(lane == (slot // sub) * bin_dev + local, lax.rem(slot, sub), places)
                label = jnp.broadcast_to(bin_ref[pl.ds(t, 1), :], (PACK, LANES))
                label = label.astype(jnp.float32).astype(jnp.bfloat16)
                steps.append(jnp.concatenate([jnp.where(label <= ids, one, zero) for ids in bin_ids], axis=0))
                chosen = slot_ids == slot
                pieces = []
                for f in range(3):
                    cells = pl.ds(pl.multiple_of(t * TILE, TILE), TILE)
                    for piece in split(field_ref[f : f + 1, cells]):
                        spread = jnp.broadcast_to(piece, (slots, LANES))
                        pieces.append(jnp.where(chosen, spread, 0.0).astype(jnp.bfloat16))
                values.append(jnp.concatenate(pieces, axis=0))
            step = jnp.concatenate(steps, axis=1)
            value = jnp.concatenate(values, axis=1)
            part = lax.dot_general(
                value, step, (((1,), (1,)), ((), ())), preferred_element_type=jnp.float32
            )
            total = part if total is None else total + part
        for f in range(3):
            running = total[2 * f * slots : (2 * f + 1) * slots] + total[(2 * f + 1) * slots : (2 * f + 2) * slots]
            for r in range(rads):
                packed = jnp.concatenate(
                    [running[a * sub : (a + 1) * sub, r * bin_dev : (r + 1) * bin_dev] for a in range(parts)], axis=1
                )
                base = (owner * rads + r) * rows + f * sub
                out_ref[pl.ds(base, sub), 0, :] = packed
        for r in range(rads):
            out_ref[(owner * rads + r) * rows + rows - 1] = places.astype(jnp.float32)


def merge_kernel(halo_dev, bin_dev, sub, rows, got_ref, mass_ref, volume_ref, entropy_ref, speed_ref):
    sources = got_ref.shape[0] // rows
    batch = math.gcd(sources, BATCH)
    row_ids = lax.broadcasted_iota(jnp.int32, (sub, LANES), 0).astype(jnp.float32)

    def add(first):
        picks, values = [], []
        for i in range(batch):
            base = (first + i) * rows
            places = jnp.broadcast_to(got_ref[base + rows - 1], (sub, LANES))
            picks.append((places == row_ids).astype(jnp.float32))
            pieces = []
            for f in range(3):
                pieces.extend(split(got_ref[pl.ds(base + f * sub, sub), 0, :]))
            values.append(jnp.concatenate(pieces, axis=1))
        pick = jnp.concatenate(picks, axis=0).astype(jnp.bfloat16)
        value = jnp.concatenate(values, axis=0).astype(jnp.bfloat16)
        return lax.dot_general(pick, value, (((0,), (0,)), ((), ())), preferred_element_type=jnp.float32)

    sums = lax.fori_loop(1, sources // batch, lambda k, acc: acc + add(k * batch), add(0))
    results = []
    for f in range(3):
        both = sums[:, 2 * f * LANES : (2 * f + 1) * LANES] + sums[:, (2 * f + 1) * LANES : (2 * f + 2) * LANES]
        acc = None
        for a in range(LANES // bin_dev):
            part = both[a * bin_dev : a * bin_dev + halo_dev, a * bin_dev : (a + 1) * bin_dev]
            acc = part if acc is None else acc + part
        results.append(acc)
    mass_ref[...], volume_ref[...], entropy_ref[...] = results
    first = lax.axis_index("rad") * bin_dev + 1
    position = (lax.broadcasted_iota(jnp.int32, (1, bin_dev), 1) + first).astype(jnp.float32)
    radius = jnp.exp(log_inner + position * (-log_inner / BINS))
    speed_ref[...] = jnp.sqrt(results[0] / radius)


def body(cell_bin, cell_fields, tile_halo, halo_owner):
    spaces = lax.axis_size("space")
    rads = lax.axis_size("rad")
    bin_dev = BINS // rads
    tiles = tile_halo.shape[0]
    halo_dev = halo_owner.shape[0] // spaces
    per = max(2, 2 * tiles // spaces)
    slots = -(-max(1, per // 2) // PACK) * PACK
    sub = slots * bin_dev // LANES
    rows = 3 * sub + 1
    vmem = pl.BlockSpec(memory_space=pltpu.VMEM)
    smem = pl.BlockSpec(memory_space=pltpu.SMEM)
    outgoing = pl.pallas_call(
        functools.partial(bin_kernel, spaces, rads, per, slots, rows),
        out_shape=jax.ShapeDtypeStruct((spaces * rads * rows, 1, LANES), jnp.float32),
        in_specs=[smem, smem, vmem, vmem],
        out_specs=vmem,
        compiler_params=pltpu.CompilerParams(vmem_limit_bytes=VMEM_LIMIT),
    )(halo_owner, tile_halo, cell_bin.reshape(tiles, TILE), cell_fields)
    received = lax.all_to_all(
        outgoing.reshape(spaces * rads, rows, 1, LANES), ("space", "rad"), split_axis=0, concat_axis=0, tiled=True
    )
    return pl.pallas_call(
        functools.partial(merge_kernel, halo_dev, bin_dev, sub, rows),
        out_shape=[jax.ShapeDtypeStruct((halo_dev, bin_dev), jnp.float32)] * 4,
        in_specs=[vmem],
        out_specs=[vmem] * 4,
        compiler_params=pltpu.CompilerParams(vmem_limit_bytes=VMEM_LIMIT),
    )(received.reshape(spaces * rads * rows, 1, LANES))


def solution(mesh):
    in_specs = (P(("space", "rad")), P(None, ("space", "rad")), P(("space", "rad")), P())
    out_specs = (P("space", "rad"), P("space", "rad"), P("space", "rad"), P("space", "rad"))
    return jax.shard_map(body, mesh=mesh, in_specs=in_specs, out_specs=out_specs, check_vma=False)
```

time: 95 us -> 29.9 us (0.31); the launches traced: 93.8 us -> 29.7 us
  waiting for transfers between devices: 28.7 us -> 0 us
  blocking collectives: 5.6 us -> 20.7 us
  matrix products: 14 us -> 0 us
  between operations: 14.1 us -> 0.66 us
  starting transfers between devices: 13.3 us -> 0 us
  local copies, waits for them, and re-layouts: 13.4 us -> 2.46 us
  Pallas kernels: 0 us -> 5.9 us
  other arithmetic: 4.6 us -> 0 us
    all_to_all x0 -> x1, blocking collectives: none -> 20.7 us  [body(): lax.all_to_all(outgoing.reshape(spaces * rads, rows, 1, LANES), ('space',...]
    unnamed x2 -> x0, waiting for transfers between devices: 18.9 us -> none
    dot_general x11 -> x0, matrix products: 14 us -> none  [the longest x8 12.4 us: one_group(): jnp.einsum('ftc,tcb->tfb', values, onehot, precision=lax.Precision.HIGHEST)]
    all_to_all x2 -> x0, starting transfers between devices: 13.3 us -> none  [the longest x1 7.28 us: body(): lax.all_to_all(slot_tags, 'space', split_axis=0, concat_axis=0, tiled=True)]
    all_to_all x2 -> x0, waiting for transfers between devices: 9.82 us -> none  [the longest x1 9.82 us: body(): lax.all_to_all(outgoing, 'space', split_axis=0, concat_axis=0, tiled=True)]
    pallas_call x0 -> x2, Pallas kernels: none -> 5.9 us  [the longest x1 4.42 us: body(): pl.pallas_call(functools.partial(bin_kernel, spaces, rads, per, slots, ro...]
    eq x9 -> x0, local copies, waits for them, and re-layouts: 5.73 us -> none  [the longest x8 5.65 us: one_group(): onehot = (labels[:, :, None] == bin_ids[None, None, :]).astype(jnp.float32)]
    all_gather x1 -> x0, blocking collectives: 5.6 us -> none  [prefix(): gathered = lax.all_gather(part, axis)]
  transfers between devices with their start and end apart: 3 -> 0, of which waited for: 2 -> 0; matrix products, arithmetic and copies ran while one was open for 22% -> 0% of each run, Pallas kernels for 0% -> 0%
where the time goes in v1:
time: 29.9 us; the launch traced here: 29.7 us
  blocking collectives  20.7 us (69%)
  Pallas kernels  5.9 us (20%)
  local copies, waits for them, and re-layouts  2.46 us (8%)
  between operations  0.66 us (2%)
    all_to_all x1, blocking collectives, body(): lax.all_to_all(outgoing.reshape(spaces * rads, rows, 1, LANES), ('space',...  20.7 us
    pallas_call x1, Pallas kernels, body(): pl.pallas_call(functools.partial(bin_kernel, spaces, rads, per, slots, ro...  4.42 us
    unnamed x8, local copies, waits for them, and re-layouts  2.46 us
    pallas_call x1, Pallas kernels, body(): pl.pallas_call(functools.partial(merge_kernel, halo_dev, bin_dev, sub, ro...  1.49 us

profile of v1, /device:TPU:0, one launch (start us, length us, event | category | flops | bytes accessed | tf_op | source)
XLA Modules:
  0.0 29.7 jit_solution(12492636641514679044)
XLA Ops:
  0.6 0.0 copy-start.2
  0.6 0.0 copy-start.3
  0.7 0.7 %copy-done.2 = s32[256]{0:T(256)S(1)} copy-done((s32[256]{0:T(256)S(1)}, s32[256]{0:T(256)}, u32[]{:S(2)}) %copy-start.2) | copy-done | bytes 1048
  1.3 0.0 copy-done.3
  1.3 0.0 copy-start
  1.3 0.9 %copy-done = f32[3,16384]{1,0:T(4,128)S(1)} copy-done((f32[3,16384]{1,0:T(4,128)S(1)}, f32[3,16384]{1,0:T(4,128)}, u32[]{:S(2)}) %copy-start) | copy-done | bytes 196632
  2.3 0.0 copy-start.1
  2.3 0.8 %copy-done.1 = s32[16384]{0:T(1024)S(1)} copy-done((s32[16384]{0:T(1024)S(1)}, s32[16384]{0:T(1024)}, u32[]{:S(2)}) %copy-start.1) | copy-done | bytes 65560
  3.1 4.4 %shard_map.75 = f32[800,1,128]{2,1,0:T(1,128)S(1)} custom-call(s32[256]{0:T(256)S(1)} %copy-done.2, s32[128]{0:T(128)S(1)} %copy-done.3, s32[128,128]{1,0:T(8,128)S(1)} %bitcast.5, f32[3,16384]{1,0:T(4,128)S(1)} %copy-done), custom_call_target="tpu_custom_call" | custom-call | tf_op jit(solution)/shard_map/pallas_call | solution.py:137
  7.5 20.7 %all_to_all.5 = f32[32,25,1,128]{3,2,1,0:T(1,128)S(1)} all-to-all(f32[32,25,1,128]{3,2,1,0:T(1,128)S(1)} %bitcast.4), channel_id=1, replica_groups=mesh['space'=8,'rad'=4] {'space','rad'}, dimensions={0} | all-to-all | bytes 819200 | tf_op jit(solution)/shard_map/all_to_all | solution.py:144
  28.2 1.5 %shard_map.76 = (f32[32,64]{1,0:T(8,128)}, f32[32,64]{1,0:T(8,128)}, f32[32,64]{1,0:T(8,128)}, f32[32,64]{1,0:T(8,128)}) custom-call(f32[800,1,128]{2,1,0:T(1,128)S(1)} %bitcast.3), custom_call_target="tpu_custom_call" | custom-call | tf_op jit(solution)/shard_map/pallas_call | solution.py:147
Async XLA Ops:
  0.6 0.7 %copy-start.2 = (s32[256]{0:T(256)S(1)}, s32[256]{0:T(256)}, u32[]{:S(2)}) copy-start(s32[256]{0:T(256)} %owner_ref.1) | copy-start | bytes 3076
  0.6 0.7 %copy-start.3 = (s32[128]{0:T(128)S(1)}, s32[128]{0:T(128)}, u32[]{:S(2)}) copy-start(s32[128]{0:T(128)} %halo_ref.1) | copy-start | bytes 1540
  1.3 1.0 %copy-start = (f32[3,16384]{1,0:T(4,128)S(1)}, f32[3,16384]{1,0:T(4,128)}, u32[]{:S(2)}) copy-start(f32[3,16384]{1,0:T(4,128)} %field_ref.1) | copy-start | bytes 589828
  2.3 0.8 %copy-start.1 = (s32[16384]{0:T(1024)S(1)}, s32[16384]{0:T(1024)}, u32[]{:S(2)}) copy-start(s32[16384]{0:T(1024)} %param.4) | copy-start | bytes 196612

commit v2 on v1

v2 whole, which is shorter than its diff:
```python
import functools
import math

import jax
import jax.numpy as jnp
from jax import lax
from jax.experimental import pallas as pl
from jax.experimental.pallas import tpu as pltpu
from jax.sharding import PartitionSpec as P

TILE = 128
BINS = 256
LANES = 128
PACK = 16
FIELDS = 4
BATCH = 32
VMEM_LIMIT = 16 * 1024 * 1024

log_inner = -2.302585092994046


def divide(x, n):
    if n & (n - 1):
        return lax.div(x, jnp.full_like(x, n)), lax.rem(x, jnp.full_like(x, n))
    return lax.shift_right_logical(x, jnp.full_like(x, n.bit_length() - 1)), x & (n - 1)


def iota(shape, dim):
    return lax.broadcasted_iota(jnp.int32, shape, dim)


def root_of(devices):
    return devices // 4 + 1


def matmul(a, b, contract):
    return lax.dot_general(a, b, ((contract, contract), ((), ())), preferred_element_type=jnp.float32)


def bin_kernel(
    spaces, rads, per, slots, rows,
    owner_hbm, halo_hbm, line_hbm, bin_hbm, field_hbm, out_ref,
    owner_ref, halo_ref, line_ref, bin_ref, field_ref, place_ref, acc_ref, sem,
):
    tiles = bin_ref.shape[0]
    halo_dev = owner_ref.shape[0] // spaces
    bin_dev = BINS // rads
    parts = LANES // bin_dev
    sub = slots // parts
    lead = FIELDS * rads
    root = root_of(spaces * rads)
    copies = [
        pltpu.make_async_copy(source, target, sem.at[k])
        for k, (source, target) in enumerate(
            [(line_hbm, line_ref), (halo_hbm, halo_ref), (owner_hbm, owner_ref), (bin_hbm, bin_ref), (field_hbm, field_ref)]
        )
    ]
    for copy in copies:
        copy.start()

    @pl.loop(0, spaces * rads)
    def _(block):
        out_ref[pl.ds(block * rows, rows - 1), :] = jnp.zeros((rows - 1, LANES), jnp.float32)
        out_ref[pl.ds(block * rows + rows - 1, 1), :] = jnp.full((1, LANES), -1.0, jnp.float32)

    for copy in copies[:1]:
        copy.wait()
    line = jnp.broadcast_to(line_ref[...], (8, tiles))
    start = (line != pltpu.roll(line, 1, 1)) | (divide(iota((8, tiles), 1), per)[1] == 0)
    start = jnp.broadcast_to(jnp.where(start, 1.0, 0.0)[:1], (tiles, tiles))
    local = jnp.broadcast_to(divide(line, halo_dev)[1].astype(jnp.float32)[:1], (tiles, tiles))
    down, across = iota((tiles, tiles), 0), iota((tiles, tiles), 1)
    before = (across <= down) & (divide(across, per)[0] == divide(down, per)[0])
    flat = jnp.concatenate([jnp.where(before, start, 0.0), jnp.where(across == down, local, 0.0)], axis=0)
    spread = lax.dot_general(
        flat.astype(jnp.bfloat16), jnp.ones((tiles, LANES), jnp.bfloat16), (((1,), (0,)), ((), ())),
        preferred_element_type=jnp.float32,
    )
    part, row = divide(spread[:tiles].astype(jnp.int32) - 1, sub)
    key = part * bin_dev + spread[tiles:].astype(jnp.int32)
    place_ref[...] = jnp.where(key == iota((tiles, LANES), 1), row, -1).astype(jnp.float32)

    one, zero = jnp.bfloat16(1), jnp.bfloat16(0)
    bin_ids = [
        (iota((PACK, LANES), 0) + k * PACK).astype(jnp.float32).astype(jnp.bfloat16) for k in range(bin_dev // PACK)
    ]
    field_id, range_id = divide(iota((lead, LANES), 0), rads)
    range_id = jnp.where(field_id < 3, range_id, -1)
    empty = jnp.zeros((2 * lead, LANES), jnp.bfloat16)

    for copy in copies[1:]:
        copy.wait()

    @pl.loop(0, tiles // per)
    def _(group):
        acc_ref[...] = jnp.zeros_like(acc_ref)
        owner = owner_ref[halo_ref[group * per]]
        slot = jnp.int32(0)
        carry = None
        width = math.gcd(per, 2)
        for first in range(0, per, width):
            values, steps = [], []
            for k in range(first, first + width):
                t = group * per + k
                span, low = divide(bin_ref[pl.ds(t, 1), :], bin_dev)
                cells = pl.ds(pl.multiple_of(t * TILE, TILE), TILE)
                field = [jnp.broadcast_to(field_ref[f : f + 1, cells], (lead, LANES)) for f in range(3)]
                value = jnp.where(field_id == 0, field[0], jnp.where(field_id == 1, field[1], field[2]))
                value = jnp.where(jnp.broadcast_to(span, (lead, LANES)) == range_id, value, 0.0)
                high = value.astype(jnp.bfloat16)
                value = jnp.concatenate([high, (value - high.astype(jnp.float32)).astype(jnp.bfloat16)], axis=0)
                values.append(jnp.concatenate([empty] * (k - first) + [value] + [empty] * (first + width - 1 - k), axis=1))
                low = jnp.broadcast_to(low, (PACK, LANES)).astype(jnp.float32).astype(jnp.bfloat16)
                steps.append(jnp.concatenate([jnp.where(low <= ids, one, zero) for ids in bin_ids], axis=0))
            sums = matmul(jnp.concatenate(values, axis=0), jnp.concatenate(steps, axis=1), (1,))
            for k in range(first, first + width):
                at = (k - first) * 2 * lead
                tile_sum = sums[at : at + lead] + sums[at + lead : at + 2 * lead]
                if k:
                    fresh = halo_ref[group * per + k] != halo_ref[group * per + k - 1]
                    slot = slot + fresh.astype(jnp.int32)
                    carry = jnp.where(fresh, 0.0, carry) + tile_sum
                else:
                    carry = tile_sum
                acc_ref[pl.ds(pl.multiple_of(slot * lead, lead), lead), :bin_dev] = carry
        base = []
        for r in range(rads):
            block = owner * rads + r
            block = jnp.where(block == 0, root, jnp.where(block == root, 0, block))
            base.append(block * rows)
            places = jnp.max(place_ref[pl.ds(group * per, per), :], axis=0, keepdims=True)
            out_ref[pl.ds(base[r] + rows - 1, 1), :] = places
        for f in range(3):
            inner = [jnp.zeros((sub, bin_dev), jnp.float32)] * parts
            for r in range(rads):
                pieces = []
                for a in range(parts):
                    own = acc_ref[pl.ds(a * sub * lead + f * rads + r, sub, stride=lead), :][:, :bin_dev]
                    pieces.append(own + inner[a])
                    inner[a] = inner[a] + jnp.broadcast_to(own[:, bin_dev - 1 :], (sub, bin_dev))
                out_ref[pl.ds(base[r] + f * sub, sub), :] = jnp.concatenate(pieces, axis=1)


def merge_kernel(halo_dev, bin_dev, sub, rows, got_ref, mass_ref, volume_ref, entropy_ref, speed_ref):
    sources = got_ref.shape[0] // rows
    batch = math.gcd(sources, BATCH)
    row_ids = iota((sub, LANES), 0).astype(jnp.float32)

    def add(first):
        picks, values = [], []
        for i in range(batch):
            base = (first + i) * rows
            places = jnp.broadcast_to(got_ref[pl.ds(base + rows - 1, 1), :], (sub, LANES))
            picks.append((places == row_ids).astype(jnp.float32))
            pieces = []
            for f in range(3):
                value = got_ref[pl.ds(base + f * sub, sub), :]
                high = value.astype(jnp.bfloat16).astype(jnp.float32)
                pieces.extend([high, value - high])
            values.append(jnp.concatenate(pieces, axis=1))
        pick = jnp.concatenate(picks, axis=0).astype(jnp.bfloat16)
        value = jnp.concatenate(values, axis=0).astype(jnp.bfloat16)
        return matmul(pick, value, (0,))

    sums = lax.fori_loop(1, sources // batch, lambda k, acc: acc + add(k * batch), add(0))
    results = []
    for f in range(3):
        both = sums[:, 2 * f * LANES : (2 * f + 1) * LANES] + sums[:, (2 * f + 1) * LANES : (2 * f + 2) * LANES]
        acc = None
        for a in range(LANES // bin_dev):
            part = both[a * bin_dev : a * bin_dev + halo_dev, a * bin_dev : (a + 1) * bin_dev]
            acc = part if acc is None else acc + part
        results.append(acc)
    mass_ref[...], volume_ref[...], entropy_ref[...] = results
    first = lax.axis_index("rad") * bin_dev + 1
    position = (iota((1, bin_dev), 1) + first).astype(jnp.float32)
    radius = jnp.exp(log_inner + position * (-log_inner / BINS))
    speed_ref[...] = jnp.sqrt(results[0] / radius)


def body(cell_bin, cell_fields, tile_halo, halo_owner):
    spaces = lax.axis_size("space")
    rads = lax.axis_size("rad")
    bin_dev = BINS // rads
    tiles = tile_halo.shape[0]
    halo_dev = halo_owner.shape[0] // spaces
    per = max(2, 2 * tiles // spaces)
    slots = -(-max(1, per // 2) // PACK) * PACK
    sub = slots * bin_dev // LANES
    rows = 3 * sub + 1
    devices = spaces * rads
    vmem = pl.BlockSpec(memory_space=pltpu.VMEM)
    hbm = pl.BlockSpec(memory_space=pltpu.HBM)
    params = pltpu.CompilerParams(vmem_limit_bytes=VMEM_LIMIT)
    outgoing = pl.pallas_call(
        functools.partial(bin_kernel, spaces, rads, per, slots, rows),
        out_shape=jax.ShapeDtypeStruct((devices * rows, LANES), jnp.float32),
        in_specs=[hbm] * 5,
        out_specs=vmem,
        scratch_shapes=[
            pltpu.SMEM(halo_owner.shape, jnp.int32),
            pltpu.SMEM((tiles,), jnp.int32),
            pltpu.VMEM((1, tiles), jnp.int32),
            pltpu.VMEM((tiles, TILE), jnp.int32),
            pltpu.VMEM(cell_fields.shape, jnp.float32),
            pltpu.VMEM((tiles, LANES), jnp.float32),
            pltpu.VMEM((slots * FIELDS * rads, LANES), jnp.float32),
            pltpu.SemaphoreType.DMA((5,)),
        ],
        compiler_params=params,
    )(
        *[
            pltpu.with_memory_space_constraint(x, pltpu.HBM)
            for x in (halo_owner, tile_halo, tile_halo.reshape(1, tiles), cell_bin.reshape(tiles, TILE), cell_fields)
        ]
    )
    order = list(range(devices))
    order[0], order[root_of(devices)] = order[root_of(devices)], order[0]
    received = lax.all_to_all(
        outgoing.reshape(devices, rows, 1, LANES),
        ("space", "rad"),
        split_axis=0,
        concat_axis=0,
        axis_index_groups=[order],
        tiled=True,
    )
    return pl.pallas_call(
        functools.partial(merge_kernel, halo_dev, bin_dev, sub, rows),
        out_shape=[jax.ShapeDtypeStruct((halo_dev, bin_dev), jnp.float32)] * 4,
        in_specs=[vmem],
        out_specs=[vmem] * 4,
        compiler_params=params,
    )(received.reshape(devices * rows, LANES))


def solution(mesh):
    in_specs = (P(("space", "rad")), P(None, ("space", "rad")), P(("space", "rad")), P())
    out_specs = (P("space", "rad"), P("space", "rad"), P("space", "rad"), P("space", "rad"))
    return jax.shard_map(body, mesh=mesh, in_specs=in_specs, out_specs=out_specs, check_vma=False)
```

time: 29.9 us -> 25 us (0.84)
  local copies, waits for them, and re-layouts: 2.46 us -> 0 us
  Pallas kernels: 5.9 us -> 3.76 us
  blocking collectives: 20.7 us -> 20.4 us
    unnamed x8 -> x0, local copies, waits for them, and re-layouts: 2.46 us -> none
    pallas_call x1, Pallas kernels: 4.42 us -> 2.85 us  [body(): pl.pallas_call(functools.partial(bin_kernel, spaces, rads, per, slots, ro...]
    pallas_call x1, Pallas kernels: 1.49 us -> 0.91 us  [body(): pl.pallas_call(functools.partial(merge_kernel, halo_dev, bin_dev, sub, ro...]
where the time goes in v2:
time: 25 us; the launch traced here: 24.8 us
  blocking collectives  20.4 us (82%)
  Pallas kernels  3.76 us (15%)
  between operations  0.64 us (3%)
    all_to_all x1, blocking collectives, body(): lax.all_to_all(outgoing.reshape(devices, rows, 1, LANES), ('space', 'rad'...  20.4 us
    pallas_call x1, Pallas kernels, body(): pl.pallas_call(functools.partial(bin_kernel, spaces, rads, per, slots, ro...  2.85 us
    pallas_call x1, Pallas kernels, body(): pl.pallas_call(functools.partial(merge_kernel, halo_dev, bin_dev, sub, ro...  0.91 us

profile of v2, /device:TPU:0, one launch (start us, length us, event | category | flops | bytes accessed | tf_op | source)
XLA Modules:
  0.0 24.8 jit_solution(17342801848866542104)
XLA Ops:
  0.6 2.9 %shard_map.75 = f32[800,128]{1,0:T(8,128)S(1)} custom-call(s32[256]{0:T(256)} %owner_hbm.1, s32[128]{0:T(128)} %halo_hbm.1, s32[1,128]{1,0:T(1,128)} %bitcast.7, s32[128,128]{1,0:T(8,128)} %bitcast.6, f32[3,16384]{1,0:T(4,128)} %field_hbm.1), custom_call_target="tpu_custom_call" | custom-call | tf_op jit(solution)/shard_map/pallas_call | solution.py:195
  3.5 20.4 %all_to_all.5 = f32[32,25,1,128]{3,2,1,0:T(1,128)S(1)} all-to-all(f32[32,25,1,128]{3,2,1,0:T(1,128)S(1)} %bitcast.5), channel_id=1, replica_groups={{9,1,2,3,4,5,6,7,8,0,10,11,12,13,14,15,16,17,18,19,20,21,22,23,24,25,26..., dimensions={0} | all-to-all | bytes 819200 | tf_op jit(solution)/shard_map/all_to_all | solution.py:219
  23.9 0.9 %shard_map.76 = (f32[32,64]{1,0:T(8,128)}, f32[32,64]{1,0:T(8,128)}, f32[32,64]{1,0:T(8,128)}, f32[32,64]{1,0:T(8,128)}) custom-call(f32[800,128]{1,0:T(8,128)S(1)} %bitcast.4), custom_call_target="tpu_custom_call" | custom-call | tf_op jit(solution)/shard_map/pallas_call | solution.py:227

commit v3 on v2

--- a/solution.py
+++ b/solution.py
@@ -29,8 +29,8 @@
     return lax.broadcasted_iota(jnp.int32, shape, dim)
 
 
-def root_of(devices):
-    return devices // 4 + 1
+def root_of(members):
+    return members - 1
 
 
 def matmul(a, b, contract):
@@ -48,7 +48,7 @@
     parts = LANES // bin_dev
     sub = slots // parts
     lead = FIELDS * rads
-    root = root_of(spaces * rads)
+    root = root_of(spaces * rads // 2)
     copies = [
         pltpu.make_async_copy(source, target, sem.at[k])
         for k, (source, target) in enumerate(
@@ -124,10 +124,11 @@
                     carry = tile_sum
                 acc_ref[pl.ds(pl.multiple_of(slot * lead, lead), lead), :bin_dev] = carry
         base = []
+        side = lax.div(owner, spaces // 2)
         for r in range(rads):
-            block = owner * rads + r
-            block = jnp.where(block == 0, root, jnp.where(block == root, 0, block))
-            base.append(block * rows)
+            place = lax.rem(owner, spaces // 2) * rads + r
+            place = jnp.where(place == root, 0, place + (place < root).astype(jnp.int32))
+            base.append((2 * place + side) * rows)
             places = jnp.max(place_ref[pl.ds(group * per, per), :], axis=0, keepdims=True)
             out_ref[pl.ds(base[r] + rows - 1, 1), :] = places
         for f in range(3):
@@ -141,15 +142,19 @@
                 out_ref[pl.ds(base[r] + f * sub, sub), :] = jnp.concatenate(pieces, axis=1)
 
 
-def merge_kernel(halo_dev, bin_dev, sub, rows, got_ref, mass_ref, volume_ref, entropy_ref, speed_ref):
-    sources = got_ref.shape[0] // rows
+def fold(x, height):
+    return jnp.concatenate([x[k : k + height] for k in range(0, x.shape[0], height)], axis=1)
+
+
+def merge_kernel(halo_dev, bin_dev, sub, rows, got_ref, own_ref, other_ref):
+    sources = got_ref.shape[0] // (2 * rows)
     batch = math.gcd(sources, BATCH)
     row_ids = iota((sub, LANES), 0).astype(jnp.float32)
 
-    def add(first):
+    def add(side, first):
         picks, values = [], []
         for i in range(batch):
-            base = (first + i) * rows
+            base = (2 * (first + i) + side) * rows
             places = jnp.broadcast_to(got_ref[pl.ds(base + rows - 1, 1), :], (sub, LANES))
             picks.append((places == row_ids).astype(jnp.float32))
             pieces = []
@@ -162,20 +167,39 @@
         value = jnp.concatenate(values, axis=0).astype(jnp.bfloat16)
         return matmul(pick, value, (0,))
 
-    sums = lax.fori_loop(1, sources // batch, lambda k, acc: acc + add(k * batch), add(0))
     results = []
-    for f in range(3):
-        both = sums[:, 2 * f * LANES : (2 * f + 1) * LANES] + sums[:, (2 * f + 1) * LANES : (2 * f + 2) * LANES]
-        acc = None
-        for a in range(LANES // bin_dev):
-            part = both[a * bin_dev : a * bin_dev + halo_dev, a * bin_dev : (a + 1) * bin_dev]
-            acc = part if acc is None else acc + part
-        results.append(acc)
-    mass_ref[...], volume_ref[...], entropy_ref[...] = results
+    for side in range(2):
+        sums = lax.fori_loop(
+            1, sources // batch, lambda k, acc, side=side: acc + add(side, k * batch), add(side, 0)
+        )
+        fields = []
+        for f in range(3):
+            both = sums[:, 2 * f * LANES : (2 * f + 1) * LANES] + sums[:, (2 * f + 1) * LANES : (2 * f + 2) * LANES]
+            acc = None
+            for a in range(LANES // bin_dev):
+                part = both[a * bin_dev : a * bin_dev + halo_dev, a * bin_dev : (a + 1) * bin_dev]
+                acc = part if acc is None else acc + part
+            fields.append(fold(acc, halo_dev // (LANES // bin_dev)))
+        results.append(jnp.concatenate(fields, axis=0))
+    first = lax.axis_index("space") < lax.axis_size("space") // 2
+    own_ref[...] = jnp.where(first, results[0], results[1])
+    other_ref[...] = jnp.where(first, results[1], results[0])
+
+
+def finish_kernel(halo_dev, bin_dev, own_ref, got_ref, mass_ref, volume_ref, entropy_ref, speed_ref):
+    total = own_ref[...] + got_ref[...]
+    height = halo_dev * bin_dev // LANES
+    total = [
+        jnp.concatenate(
+            [total[f * height : (f + 1) * height, a : a + bin_dev] for a in range(0, LANES, bin_dev)], axis=0
+        )
+        for f in range(3)
+    ]
+    mass_ref[...], volume_ref[...], entropy_ref[...] = total
     first = lax.axis_index("rad") * bin_dev + 1
     position = (iota((1, bin_dev), 1) + first).astype(jnp.float32)
     radius = jnp.exp(log_inner + position * (-log_inner / BINS))
-    speed_ref[...] = jnp.sqrt(results[0] / radius)
+    speed_ref[...] = jnp.sqrt(total[0] / radius)
 
 
 def body(cell_bin, cell_fields, tile_halo, halo_owner):
@@ -214,23 +238,31 @@
             for x in (halo_owner, tile_halo, tile_halo.reshape(1, tiles), cell_bin.reshape(tiles, TILE), cell_fields)
         ]
     )
-    order = list(range(devices))
-    order[0], order[root_of(devices)] = order[root_of(devices)], order[0]
+    root = root_of(devices // 2)
+    order = [root] + [k for k in range(devices // 2) if k != root]
     received = lax.all_to_all(
-        outgoing.reshape(devices, rows, 1, LANES),
+        outgoing.reshape(devices // 2, 2 * rows, 1, LANES),
         ("space", "rad"),
         split_axis=0,
         concat_axis=0,
-        axis_index_groups=[order],
+        axis_index_groups=[[side * (devices // 2) + k for k in order] for side in range(2)],
         tiled=True,
     )
+    own, other = pl.pallas_call(
+        functools.partial(merge_kernel, halo_dev, bin_dev, sub, rows),
+        out_shape=[jax.ShapeDtypeStruct((3 * halo_dev * bin_dev // LANES, LANES), jnp.float32)] * 2,
+        in_specs=[vmem],
+        out_specs=[vmem] * 2,
+        compiler_params=params,
+    )(received.reshape(devices * rows, LANES))
+    got = lax.ppermute(other, "space", [(s, (s + spaces // 2) % spaces) for s in range(spaces)])
     return pl.pallas_call(
-        functools.partial(merge_kernel, halo_dev, bin_dev, sub, rows),
+        functools.partial(finish_kernel, halo_dev, bin_dev),
         out_shape=[jax.ShapeDtypeStruct((halo_dev, bin_dev), jnp.float32)] * 4,
-        in_specs=[vmem],
+        in_specs=[vmem] * 2,
         out_specs=[vmem] * 4,
         compiler_params=params,
-    )(received.reshape(devices * rows, LANES))
+    )(own, got)
 
 
 def solution(mesh):

time: 25 us -> 22.3 us (0.89)
  blocking collectives: 20.4 us -> 12.8 us
  starting transfers between devices: 0 us -> 2.64 us
  waiting for transfers between devices: 0 us -> 2.13 us
    all_to_all x1, blocking collectives: 20.4 us -> 12.8 us  [body(): lax.all_to_all(outgoing.reshape(devices // 2, 2 * rows, 1, LANES), ('spac...]
    ppermute x0 -> x1, starting transfers between devices: none -> 2.64 us  [body(): lax.ppermute(other, 'space', [(s, (s + spaces // 2) % spaces) for s in ra...]
    ppermute x0 -> x1, waiting for transfers between devices: none -> 2.13 us  [body(): lax.ppermute(other, 'space', [(s, (s + spaces // 2) % spaces) for s in ra...]
    pallas_call x0 -> x1, Pallas kernels: none -> 0.69 us  [body(): pl.pallas_call(functools.partial(finish_kernel, halo_dev, bin_dev), out_s...]
    pallas_call x1, Pallas kernels: 0.91 us -> 0.42 us  [body(): pl.pallas_call(functools.partial(merge_kernel, halo_dev, bin_dev, sub, ro...]
  transfers between devices with their start and end apart: 0 -> 1, of which waited for: 0 -> 1; matrix products, arithmetic and copies ran while one was open for 0% -> 0% of each run, Pallas kernels for 0% -> 0%
where the time goes in v3:
time: 22.3 us; the launch traced here: 22.2 us
  blocking collectives  12.8 us (57%)
  Pallas kernels  3.97 us (18%)
  starting transfers between devices  2.64 us (12%)
  waiting for transfers between devices  2.13 us (10%)
  between operations  0.64 us (3%)
    all_to_all x1, blocking collectives, body(): lax.all_to_all(outgoing.reshape(devices // 2, 2 * rows, 1, LANES), ('spac...  12.8 us
    pallas_call x1, Pallas kernels, body(): pl.pallas_call(functools.partial(bin_kernel, spaces, rads, per, slots, ro...  2.86 us
    ppermute x1, starting transfers between devices, body(): lax.ppermute(other, 'space', [(s, (s + spaces // 2) % spaces) for s in ra...  2.64 us
    ppermute x1, waiting for transfers between devices, body(): lax.ppermute(other, 'space', [(s, (s + spaces // 2) % spaces) for s in ra...  2.13 us
    pallas_call x1, Pallas kernels, body(): pl.pallas_call(functools.partial(finish_kernel, halo_dev, bin_dev), out_s...  0.69 us
  transfers between devices with their start and end apart: 1, of which 1 were waited for; matrix products, arithmetic and copies ran while one was open for 0% of the time, Pallas kernels for 0%

profile of v3, /device:TPU:0, one launch (start us, length us, event | category | flops | bytes accessed | tf_op | source)
XLA Modules:
  0.0 22.2 jit_solution(12894089385401528738)
XLA Ops:
  0.6 2.9 %shard_map.75 = f32[800,128]{1,0:T(8,128)S(1)} custom-call(s32[256]{0:T(256)} %owner_hbm.1, s32[128]{0:T(128)} %halo_hbm.1, s32[1,128]{1,0:T(1,128)} %bitcast.7, s32[128,128]{1,0:T(8,128)} %bitcast.6, f32[3,16384]{1,0:T(4,128)} %field_hbm.1), custom_call_target="tpu_custom_call" | custom-call | tf_op jit(solution)/shard_map/pallas_call | solution.py:219
  3.5 12.8 %all_to_all.5 = f32[16,50,1,128]{3,2,1,0:T(1,128)S(1)} all-to-all(f32[16,50,1,128]{3,2,1,0:T(1,128)S(1)} %bitcast.5), channel_id=1, replica_groups={{15,0,1,2,3,4,5,6,7,8,9,10,11,12,13,14},{31,16,17,18,19,20,21,22,23,24,..., dimensions={0} | all-to-all | bytes 819200 | tf_op jit(solution)/shard_map/all_to_all | solution.py:243
  16.3 0.4 %shard_map.76 = (f32[48,128]{1,0:T(8,128)S(1)}, f32[48,128]{1,0:T(8,128)S(1)}) custom-call(f32[800,128]{1,0:T(8,128)S(1)} %bitcast.4), custom_call_target="tpu_custom_call" | custom-call | tf_op jit(solution)/shard_map/pallas_call | solution.py:251
  16.7 2.6 %collective-permute-start = (f32[48,128]{1,0:T(8,128)S(1)}, f32[48,128]{1,0:T(8,128)S(1)}, u32[]{:S(2)}, u32[]{:S(2)}) collective-permute-start(f32[48,128]{1,0:T(8,128)S(1)} %get-tuple-element.7), channel_id=1, source_target_pairs={{0,16},{4,20},{8,24},{12,28},{16,0},{20,4},{24,8},{28,12},{1,17},{... | collective-permute-start | bytes 73736 | tf_op jit(solution)/shard_map/ppermute | solution.py:258
  19.3 2.1 %collective-permute-done.got_ref = f32[48,128]{1,0:T(8,128)S(1)} collective-permute-done((f32[48,128]{1,0:T(8,128)S(1)}, f32[48,128]{1,0:T(8,128)S(1)}, u32[]{:S(2)}, u32[]{:S(2)}) %collective-permute-start) | collective-permute-done | bytes 24608 | tf_op jit(solution)/shard_map/ppermute | solution.py:258
  21.5 0.7 %shard_map.77 = (f32[32,64]{1,0:T(8,128)}, f32[32,64]{1,0:T(8,128)}, f32[32,64]{1,0:T(8,128)}, f32[32,64]{1,0:T(8,128)}) custom-call(f32[48,128]{1,0:T(8,128)S(1)} %get-tuple-element.6.own_ref, f32[48,128]{1,0:T(8,128)S(1)} %collective-permute-done.got_ref), custom_call_target="tpu_custom_call" | custom-call | tf_op jit(solution)/shard_map/pallas_call | solution.py:259
Async XLA Ops:
  16.7 4.8 %collective-permute-start = (f32[48,128]{1,0:T(8,128)S(1)}, f32[48,128]{1,0:T(8,128)S(1)}, u32[]{:S(2)}, u32[]{:S(2)}) collective-permute-start(f32[48,128]{1,0:T(8,128)S(1)} %get-tuple-element.7), channel_id=1, source_target_pairs={{0,16},{4,20},{8,24},{12,28},{16,0},{20,4},{24,8},{28,12},{1,17},{... | collective-permute-start | bytes 73736 | tf_op jit(solution)/shard_map/ppermute | solution.py:258

commit v4 on v3

--- a/solution.py
+++ b/solution.py
@@ -13,6 +13,7 @@
 LANES = 128
 PACK = 16
 FIELDS = 4
+UNROLL = 4
 BATCH = 32
 VMEM_LIMIT = 16 * 1024 * 1024
 
@@ -27,10 +28,6 @@
 
 def iota(shape, dim):
     return lax.broadcasted_iota(jnp.int32, shape, dim)
-
-
-def root_of(members):
-    return members - 1
 
 
 def matmul(a, b, contract):
@@ -48,7 +45,6 @@
     parts = LANES // bin_dev
     sub = slots // parts
     lead = FIELDS * rads
-    root = root_of(spaces * rads // 2)
     copies = [
         pltpu.make_async_copy(source, target, sem.at[k])
         for k, (source, target) in enumerate(
@@ -91,8 +87,7 @@
     for copy in copies[1:]:
         copy.wait()
 
-    @pl.loop(0, tiles // per)
-    def _(group):
+    def one_group(group, acc_ref):
         acc_ref[...] = jnp.zeros_like(acc_ref)
         owner = owner_ref[halo_ref[group * per]]
         slot = jnp.int32(0)
@@ -125,9 +120,10 @@
                 acc_ref[pl.ds(pl.multiple_of(slot * lead, lead), lead), :bin_dev] = carry
         base = []
         side = lax.div(owner, spaces // 2)
+        half = lax.div(lax.axis_index("space"), spaces // 2)
         for r in range(rads):
-            place = lax.rem(owner, spaces // 2) * rads + r
-            place = jnp.where(place == root, 0, place + (place < root).astype(jnp.int32))
+            place = lax.rem(owner, spaces // 2) * rads + jnp.where(side == half, r, r ^ 1)
+            place = spaces // 2 * rads - 1 - place
             base.append((2 * place + side) * rows)
             places = jnp.max(place_ref[pl.ds(group * per, per), :], axis=0, keepdims=True)
             out_ref[pl.ds(base[r] + rows - 1, 1), :] = places
@@ -140,6 +136,14 @@
                     pieces.append(own + inner[a])
                     inner[a] = inner[a] + jnp.broadcast_to(own[:, bin_dev - 1 :], (sub, bin_dev))
                 out_ref[pl.ds(base[r] + f * sub, sub), :] = jnp.concatenate(pieces, axis=1)
+
+    unrolled = acc_ref.shape[0]
+    for group in range(unrolled):
+        one_group(group, acc_ref.at[group])
+
+    @pl.loop(unrolled, tiles // per)
+    def _(group):
+        one_group(group, acc_ref.at[0])
 
 
 def fold(x, height):
@@ -228,7 +232,7 @@
             pltpu.VMEM((tiles, TILE), jnp.int32),
             pltpu.VMEM(cell_fields.shape, jnp.float32),
             pltpu.VMEM((tiles, LANES), jnp.float32),
-            pltpu.VMEM((slots * FIELDS * rads, LANES), jnp.float32),
+            pltpu.VMEM((min(UNROLL, tiles // per), slots * FIELDS * rads, LANES), jnp.float32),
             pltpu.SemaphoreType.DMA((5,)),
         ],
         compiler_params=params,
@@ -238,8 +242,7 @@
             for x in (halo_owner, tile_halo, tile_halo.reshape(1, tiles), cell_bin.reshape(tiles, TILE), cell_fields)
         ]
     )
-    root = root_of(devices // 2)
-    order = [root] + [k for k in range(devices // 2) if k != root]
+    order = range(devices // 2 - 1, -1, -1)
     received = lax.all_to_all(
         outgoing.reshape(devices // 2, 2 * rows, 1, LANES),
         ("space", "rad"),
@@ -255,7 +258,8 @@
         out_specs=[vmem] * 2,
         compiler_params=params,
     )(received.reshape(devices * rows, LANES))
-    got = lax.ppermute(other, "space", [(s, (s + spaces // 2) % spaces) for s in range(spaces)])
+    partners = [(d, (d + devices // 2) % devices ^ 1) for d in range(devices)]
+    got = lax.ppermute(other, ("space", "rad"), partners)
     return pl.pallas_call(
         functools.partial(finish_kernel, halo_dev, bin_dev),
         out_shape=[jax.ShapeDtypeStruct((halo_dev, bin_dev), jnp.float32)] * 4,

time: 22.3 us -> 20.9 us (0.937)
  Pallas kernels: 3.97 us -> 3.22 us
  waiting for transfers between devices: 2.13 us -> 1.52 us
  blocking collectives: 12.8 us -> 12.4 us
  starting transfers between devices: 2.64 us -> 2.94 us
    pallas_call x1, Pallas kernels: 2.86 us -> 2.11 us  [body(): pl.pallas_call(functools.partial(bin_kernel, spaces, rads, per, slots, ro...]
    ppermute x1, waiting for transfers between devices: 2.13 us -> 1.52 us  [body(): got = lax.ppermute(other, ('space', 'rad'), partners)]
    all_to_all x1, blocking collectives: 12.8 us -> 12.4 us  [body(): lax.all_to_all(outgoing.reshape(devices // 2, 2 * rows, 1, LANES), ('spac...]
    ppermute x1, starting transfers between devices: 2.64 us -> 2.94 us  [body(): got = lax.ppermute(other, ('space', 'rad'), partners)]
where the time goes in v4:
time: 20.9 us; the launch traced here: 20.7 us
  blocking collectives  12.4 us (59%)
  Pallas kernels  3.22 us (15%)
  starting transfers between devices  2.94 us (14%)
  waiting for transfers between devices  1.52 us (7%)
  between operations  0.64 us (3%)
    all_to_all x1, blocking collectives, body(): lax.all_to_all(outgoing.reshape(devices // 2, 2 * rows, 1, LANES), ('spac...  12.4 us
    ppermute x1, starting transfers between devices, body(): got = lax.ppermute(other, ('space', 'rad'), partners)  2.94 us
    pallas_call x1, Pallas kernels, body(): pl.pallas_call(functools.partial(bin_kernel, spaces, rads, per, slots, ro...  2.11 us
    ppermute x1, waiting for transfers between devices, body(): got = lax.ppermute(other, ('space', 'rad'), partners)  1.52 us
    pallas_call x1, Pallas kernels, body(): pl.pallas_call(functools.partial(finish_kernel, halo_dev, bin_dev), out_s...  0.69 us
  transfers between devices with their start and end apart: 1, of which 1 were waited for; matrix products, arithmetic and copies ran while one was open for 0% of the time, Pallas kernels for 0%

profile of v4, /device:TPU:0, one launch (start us, length us, event | category | flops | bytes accessed | tf_op | source)
XLA Modules:
  0.0 20.7 jit_solution(11184588105414072100)
XLA Ops:
  0.6 2.1 %shard_map.75 = f32[800,128]{1,0:T(8,128)S(1)} custom-call(s32[256]{0:T(256)} %owner_hbm.1, s32[128]{0:T(128)} %halo_hbm.1, s32[1,128]{1,0:T(1,128)} %bitcast.7, s32[128,128]{1,0:T(8,128)} %bitcast.6, f32[3,16384]{1,0:T(4,128)} %field_hbm.1), custom_call_target="tpu_custom_call" | custom-call | tf_op jit(solution)/shard_map/pallas_call | solution.py:223
  2.7 12.4 %all_to_all.5 = f32[16,50,1,128]{3,2,1,0:T(1,128)S(1)} all-to-all(f32[16,50,1,128]{3,2,1,0:T(1,128)S(1)} %bitcast.5), channel_id=1, replica_groups={{15,14,13,12,11,10,9,8,7,6,5,4,3,2,1,0},{31,30,29,28,27,26,25,24,23,22,..., dimensions={0} | all-to-all | bytes 819200 | tf_op jit(solution)/shard_map/all_to_all | solution.py:246
  15.1 0.4 %shard_map.76 = (f32[48,128]{1,0:T(8,128)S(1)}, f32[48,128]{1,0:T(8,128)S(1)}) custom-call(f32[800,128]{1,0:T(8,128)S(1)} %bitcast.4), custom_call_target="tpu_custom_call" | custom-call | tf_op jit(solution)/shard_map/pallas_call | solution.py:254
  15.5 2.9 %collective-permute-start = (f32[48,128]{1,0:T(8,128)S(1)}, f32[48,128]{1,0:T(8,128)S(1)}, u32[]{:S(2)}, u32[]{:S(2)}) collective-permute-start(f32[48,128]{1,0:T(8,128)S(1)} %get-tuple-element.7), channel_id=1, source_target_pairs={{0,17},{1,16},{2,19},{3,18},{4,21},{5,20},{6,23},{7,22},{8,25},{9,... | collective-permute-start | bytes 73736 | tf_op jit(solution)/shard_map/ppermute | solution.py:262
  18.5 1.5 %collective-permute-done.got_ref = f32[48,128]{1,0:T(8,128)S(1)} collective-permute-done((f32[48,128]{1,0:T(8,128)S(1)}, f32[48,128]{1,0:T(8,128)S(1)}, u32[]{:S(2)}, u32[]{:S(2)}) %collective-permute-start) | collective-permute-done | bytes 24608 | tf_op jit(solution)/shard_map/ppermute | solution.py:262
  20.0 0.7 %shard_map.77 = (f32[32,64]{1,0:T(8,128)}, f32[32,64]{1,0:T(8,128)}, f32[32,64]{1,0:T(8,128)}, f32[32,64]{1,0:T(8,128)}) custom-call(f32[48,128]{1,0:T(8,128)S(1)} %get-tuple-element.6.own_ref, f32[48,128]{1,0:T(8,128)S(1)} %collective-permute-done.got_ref), custom_call_target="tpu_custom_call" | custom-call | tf_op jit(solution)/shard_map/pallas_call | solution.py:263
Async XLA Ops:
  15.5 4.5 %collective-permute-start = (f32[48,128]{1,0:T(8,128)S(1)}, f32[48,128]{1,0:T(8,128)S(1)}, u32[]{:S(2)}, u32[]{:S(2)}) collective-permute-start(f32[48,128]{1,0:T(8,128)S(1)} %get-tuple-element.7), channel_id=1, source_target_pairs={{0,17},{1,16},{2,19},{3,18},{4,21},{5,20},{6,23},{7,22},{8,25},{9,... | collective-permute-start | bytes 73736 | tf_op jit(solution)/shard_map/ppermute | solution.py:262

commit v5 on v4

--- a/solution.py
+++ b/solution.py
@@ -37,7 +37,7 @@
 def bin_kernel(
     spaces, rads, per, slots, rows,
     owner_hbm, halo_hbm, line_hbm, bin_hbm, field_hbm, out_ref,
-    owner_ref, halo_ref, line_ref, bin_ref, field_ref, place_ref, acc_ref, sem,
+    owner_ref, halo_ref, line_ref, bin_ref, span_ref, low_ref, field_ref, place_ref, acc_ref, sem,
 ):
     tiles = bin_ref.shape[0]
     halo_dev = owner_ref.shape[0] // spaces
@@ -73,19 +73,20 @@
         preferred_element_type=jnp.float32,
     )
     part, row = divide(spread[:tiles].astype(jnp.int32) - 1, sub)
-    key = part * bin_dev + spread[tiles:].astype(jnp.int32)
+    key = part * halo_dev + spread[tiles:].astype(jnp.int32)
     place_ref[...] = jnp.where(key == iota((tiles, LANES), 1), row, -1).astype(jnp.float32)
 
     one, zero = jnp.bfloat16(1), jnp.bfloat16(0)
     bin_ids = [
         (iota((PACK, LANES), 0) + k * PACK).astype(jnp.float32).astype(jnp.bfloat16) for k in range(bin_dev // PACK)
     ]
-    field_id, range_id = divide(iota((lead, LANES), 0), rads)
-    range_id = jnp.where(field_id < 3, range_id, -1)
+    field_id, range_id = divide(iota((2 * rads, LANES), 0), rads)
     empty = jnp.zeros((2 * lead, LANES), jnp.bfloat16)
 
     for copy in copies[1:]:
         copy.wait()
+    span_ref[...], low = divide(bin_ref[...], bin_dev)
+    low_ref[...] = low.astype(jnp.float32)
 
     def one_group(group, acc_ref):
         acc_ref[...] = jnp.zeros_like(acc_ref)
@@ -97,15 +98,16 @@
             values, steps = [], []
             for k in range(first, first + width):
                 t = group * per + k
-                span, low = divide(bin_ref[pl.ds(t, 1), :], bin_dev)
+                span, low = span_ref[pl.ds(t, 1), :], low_ref[pl.ds(t, 1), :]
                 cells = pl.ds(pl.multiple_of(t * TILE, TILE), TILE)
-                field = [jnp.broadcast_to(field_ref[f : f + 1, cells], (lead, LANES)) for f in range(3)]
-                value = jnp.where(field_id == 0, field[0], jnp.where(field_id == 1, field[1], field[2]))
-                value = jnp.where(jnp.broadcast_to(span, (lead, LANES)) == range_id, value, 0.0)
+                field = [jnp.broadcast_to(field_ref[f : f + 1, cells], (2 * rads, LANES)) for f in range(3)]
+                inside = jnp.broadcast_to(span, (2 * rads, LANES)) == range_id
+                value = [jnp.where(field_id == 0, field[0], field[1]), field[2]]
+                value = jnp.concatenate([jnp.where(inside, v, 0.0) for v in value], axis=0)
                 high = value.astype(jnp.bfloat16)
                 value = jnp.concatenate([high, (value - high.astype(jnp.float32)).astype(jnp.bfloat16)], axis=0)
                 values.append(jnp.concatenate([empty] * (k - first) + [value] + [empty] * (first + width - 1 - k), axis=1))
-                low = jnp.broadcast_to(low, (PACK, LANES)).astype(jnp.float32).astype(jnp.bfloat16)
+                low = jnp.broadcast_to(low, (PACK, LANES)).astype(jnp.bfloat16)
                 steps.append(jnp.concatenate([jnp.where(low <= ids, one, zero) for ids in bin_ids], axis=0))
             sums = matmul(jnp.concatenate(values, axis=0), jnp.concatenate(steps, axis=1), (1,))
             for k in range(first, first + width):
@@ -153,6 +155,7 @@
 def merge_kernel(halo_dev, bin_dev, sub, rows, got_ref, own_ref, other_ref):
     sources = got_ref.shape[0] // (2 * rows)
     batch = math.gcd(sources, BATCH)
+    parts = LANES // bin_dev
     row_ids = iota((sub, LANES), 0).astype(jnp.float32)
 
     def add(side, first):
@@ -160,7 +163,7 @@
         for i in range(batch):
             base = (2 * (first + i) + side) * rows
             places = jnp.broadcast_to(got_ref[pl.ds(base + rows - 1, 1), :], (sub, LANES))
-            picks.append((places == row_ids).astype(jnp.float32))
+            picks.append((places == row_ids).astype(jnp.float32)[:, : parts * halo_dev])
             pieces = []
             for f in range(3):
                 value = got_ref[pl.ds(base + f * sub, sub), :]
@@ -180,8 +183,8 @@
         for f in range(3):
             both = sums[:, 2 * f * LANES : (2 * f + 1) * LANES] + sums[:, (2 * f + 1) * LANES : (2 * f + 2) * LANES]
             acc = None
-            for a in range(LANES // bin_dev):
-                part = both[a * bin_dev : a * bin_dev + halo_dev, a * bin_dev : (a + 1) * bin_dev]
+            for a in range(parts):
+                part = both[a * halo_dev : (a + 1) * halo_dev, a * bin_dev : (a + 1) * bin_dev]
                 acc = part if acc is None else acc + part
             fields.append(fold(acc, halo_dev // (LANES // bin_dev)))
         results.append(jnp.concatenate(fields, axis=0))
@@ -230,6 +233,8 @@
             pltpu.SMEM((tiles,), jnp.int32),
             pltpu.VMEM((1, tiles), jnp.int32),
             pltpu.VMEM((tiles, TILE), jnp.int32),
+            pltpu.VMEM((tiles, TILE), jnp.int32),
+            pltpu.VMEM((tiles, TILE), jnp.float32),
             pltpu.VMEM(cell_fields.shape, jnp.float32),
             pltpu.VMEM((tiles, LANES), jnp.float32),
             pltpu.VMEM((min(UNROLL, tiles // per), slots * FIELDS * rads, LANES), jnp.float32),

time: 20.9 us -> 20.8 us (level)
  no operation moved by 1% of the time
where the time goes in v5:
time: 20.8 us; the launch traced here: 20.6 us
  blocking collectives  12.4 us (60%)
  Pallas kernels  3.11 us (15%)
  starting transfers between devices  2.95 us (14%)
  waiting for transfers between devices  1.52 us (7%)
  between operations  0.64 us (3%)
    all_to_all x1, blocking collectives, body(): lax.all_to_all(outgoing.reshape(devices // 2, 2 * rows, 1, LANES), ('spac...  12.4 us
    ppermute x1, starting transfers between devices, body(): got = lax.ppermute(other, ('space', 'rad'), partners)  2.95 us
    pallas_call x1, Pallas kernels, body(): pl.pallas_call(functools.partial(bin_kernel, spaces, rads, per, slots, ro...  2.04 us
    ppermute x1, waiting for transfers between devices, body(): got = lax.ppermute(other, ('space', 'rad'), partners)  1.52 us
    pallas_call x1, Pallas kernels, body(): pl.pallas_call(functools.partial(finish_kernel, halo_dev, bin_dev), out_s...  0.69 us
  transfers between devices with their start and end apart: 1, of which 1 were waited for; matrix products, arithmetic and copies ran while one was open for 0% of the time, Pallas kernels for 0%

profile of v5, /device:TPU:0, one launch (start us, length us, event | category | flops | bytes accessed | tf_op | source)
XLA Modules:
  0.0 20.6 jit_solution(12677083603255127170)
XLA Ops:
  0.6 2.0 %shard_map.75 = f32[800,128]{1,0:T(8,128)S(1)} custom-call(s32[256]{0:T(256)} %owner_hbm.1, s32[128]{0:T(128)} %halo_hbm.1, s32[1,128]{1,0:T(1,128)} %bitcast.7, s32[128,128]{1,0:T(8,128)} %bitcast.6, f32[3,16384]{1,0:T(4,128)} %field_hbm.1), custom_call_target="tpu_custom_call" | custom-call | tf_op jit(solution)/shard_map/pallas_call | solution.py:226
  2.7 12.4 %all_to_all.5 = f32[16,50,1,128]{3,2,1,0:T(1,128)S(1)} all-to-all(f32[16,50,1,128]{3,2,1,0:T(1,128)S(1)} %bitcast.5), channel_id=1, replica_groups={{15,14,13,12,11,10,9,8,7,6,5,4,3,2,1,0},{31,30,29,28,27,26,25,24,23,22,..., dimensions={0} | all-to-all | bytes 819200 | tf_op jit(solution)/shard_map/all_to_all | solution.py:251
  15.0 0.4 %shard_map.76 = (f32[48,128]{1,0:T(8,128)S(1)}, f32[48,128]{1,0:T(8,128)S(1)}) custom-call(f32[800,128]{1,0:T(8,128)S(1)} %bitcast.4), custom_call_target="tpu_custom_call" | custom-call | tf_op jit(solution)/shard_map/pallas_call | solution.py:259
  15.4 3.0 %collective-permute-start = (f32[48,128]{1,0:T(8,128)S(1)}, f32[48,128]{1,0:T(8,128)S(1)}, u32[]{:S(2)}, u32[]{:S(2)}) collective-permute-start(f32[48,128]{1,0:T(8,128)S(1)} %get-tuple-element.7), channel_id=1, source_target_pairs={{0,17},{1,16},{2,19},{3,18},{4,21},{5,20},{6,23},{7,22},{8,25},{9,... | collective-permute-start | bytes 73736 | tf_op jit(solution)/shard_map/ppermute | solution.py:267
  18.4 1.5 %collective-permute-done.got_ref = f32[48,128]{1,0:T(8,128)S(1)} collective-permute-done((f32[48,128]{1,0:T(8,128)S(1)}, f32[48,128]{1,0:T(8,128)S(1)}, u32[]{:S(2)}, u32[]{:S(2)}) %collective-permute-start) | collective-permute-done | bytes 24608 | tf_op jit(solution)/shard_map/ppermute | solution.py:267
  19.9 0.7 %shard_map.77 = (f32[32,64]{1,0:T(8,128)}, f32[32,64]{1,0:T(8,128)}, f32[32,64]{1,0:T(8,128)}, f32[32,64]{1,0:T(8,128)}) custom-call(f32[48,128]{1,0:T(8,128)S(1)} %get-tuple-element.6.own_ref, f32[48,128]{1,0:T(8,128)S(1)} %collective-permute-done.got_ref), custom_call_target="tpu_custom_call" | custom-call | tf_op jit(solution)/shard_map/pallas_call | solution.py:268
Async XLA Ops:
  15.4 4.5 %collective-permute-start = (f32[48,128]{1,0:T(8,128)S(1)}, f32[48,128]{1,0:T(8,128)S(1)}, u32[]{:S(2)}, u32[]{:S(2)}) collective-permute-start(f32[48,128]{1,0:T(8,128)S(1)} %get-tuple-element.7), channel_id=1, source_target_pairs={{0,17},{1,16},{2,19},{3,18},{4,21},{5,20},{6,23},{7,22},{8,25},{9,... | collective-permute-start | bytes 73736 | tf_op jit(solution)/shard_map/ppermute | solution.py:267
